TPU v7x, 512 devices: a whole 4x4x16 slice. The times are simulated.
512 devices in a mesh: dp: 2 (over y_lo), ctx: 16 (over y_hi, x, core), tensor: 16 (over z).
Axes of the slice: x: 4, y: 4 (y_hi: 2, y_lo: 2; y = y_hi * 2 + y_lo), z: 16, core: 2. Of those that a mesh axis runs over, the one named last changes fastest.
Arguments:
- residual: bfloat16 [8192, 3584], P(('dp', 'ctx', 'tensor')), parts along dimension 0, may hold values from -6 to 6
- queries: bfloat16 [8192, 4096], P(('dp', 'ctx'), 'tensor'), parts along dimension 0, may hold values from -8 to 8
- key_heads: bfloat16 [8192, 2048], P(('dp', 'ctx'), 'tensor'), parts along dimension 0, may hold values from -8 to 8
- value_heads: bfloat16 [8192, 2048], P(('dp', 'ctx'), 'tensor'), parts along dimension 0, may hold values from -6 to 6
- doc_blocks: int32 [12], P('dp'), parts along dimension 0, may hold values from 1 to 64, 128 in all
- out_weight: bfloat16 [4096, 3584], P('tensor'), may hold values from -0.265625 to 0.265625
- post_gain: float32 [3584], replicated, may hold values from 0.1 to 1.9
- ffn_gain: float32 [3584], replicated, may hold values from 0.1 to 1.9
- gate_weight: bfloat16 [3584, 14336], P('ctx', 'tensor'), may hold values from -0.09375 to 0.09375
- up_weight: bfloat16 [3584, 14336], P('ctx', 'tensor'), may hold values from -0.09375 to 0.09375
Outputs:
- mixed_stream: bfloat16 [8192, 3584], P(('dp', 'ctx', 'tensor')), parts along dimension 0
- ffn_hidden: bfloat16 [8192, 14336], P(('dp', 'ctx'), 'tensor'), parts along dimension 0
There are 2 independent parts, one for each index of `dp`. A program takes and returns all parts, laid end to end along the dimension named above; an argument that names none is the same for every part. Nothing has to cross between parts.
Inputs may be any that keep to these rules, and one draw needn't show every extreme that they name: `doc_blocks`: the lengths, in blocks of 32 positions, of the 6 documents packed in order into the sequence; they sum to 128, and the longest has exactly 64 blocks.
All inputs are finite; a program needn't handle non-finite values.
Results may differ from a plain program's by a relative error of at most 0.025.
Values may be sent and summed in bfloat16 or wider, within the bound.
A program may use at most 64 MiB of HBM per device.

v0:
```python
import jax
import jax.numpy as jnp
from jax import lax
from jax.sharding import PartitionSpec as P

BLOCK = 32


SOFT_CAP = 50.0
NORM_EPS = 1e-06
ROPE_BASE = 10000.0


def partner_2(value, axis, apart):
    mask = 2**apart
    pairs = [(source, source ^ mask) for source in range(lax.axis_size(axis))]
    return lax.ppermute(value, axis, pairs)


def in_one_piece(arrays, axis, dim, along):
    both = jnp.concatenate(arrays, axis=along)
    out, at, done = (lax.all_gather(both, axis, axis=dim, tiled=True), 0, [])
    for a in arrays:
        done.append(lax.slice_in_dim(out, at, at + a.shape[along], axis=along))
        at += a.shape[along]
    return tuple(done)


def split_up(array, dim, peers):
    before, after = (array.shape[:dim], array.shape[dim + 1 :])
    return jnp.moveaxis(array.reshape(*before, peers, -1, *after), dim, 0)


def sent_and_summed(array, axis, dim):
    peers = lax.axis_size(axis)
    blocks = lax.all_to_all(split_up(array, dim, peers), axis, 0, 0, tiled=True)
    return jnp.sum(blocks.astype(jnp.float32), axis=0)


def in_order(blocks, dim):
    dims = list(blocks.shape[1:])
    dims[dim] *= blocks.shape[0]
    return jnp.moveaxis(blocks, 0, dim).reshape(dims)


def sent_to_all(array, axis):
    peers = lax.axis_size(axis)
    return lax.all_to_all(
        jnp.broadcast_to(array[None], (peers, *array.shape)), axis, 0, 0, tiled=True
    )


def collect(array, axis, dim):
    return in_order(sent_to_all(array, axis), dim)


def rope_angles(positions, head_size):
    halfway = head_size // 2
    frequency = ROPE_BASE ** (-(jnp.arange(halfway, dtype=jnp.float32) * 2.0) / head_size)
    angles = positions.astype(jnp.float32)[:, None] * frequency[None, :]
    return (jnp.cos(angles), jnp.sin(angles))


def rotate(heads_in, cosine, sine_value, head_size):
    rows_here = heads_in.shape[0]
    reshaped = heads_in.astype(jnp.float32).reshape(rows_here, -1, head_size)
    leading = reshaped[:, :, : head_size // 2]
    trailing = reshaped[:, :, head_size // 2 :]
    cos_wide = cosine[:, None, :]
    sin_wide = sine_value[:, None, :]
    turned = jnp.concatenate(
        [leading * cos_wide - trailing * sin_wide, trailing * cos_wide + leading * sin_wide], axis=2
    )
    return turned.reshape(rows_here, -1).astype(jnp.bfloat16)


def doc_of(positions, doc_blocks):
    doc_ends = jnp.cumsum(doc_blocks)
    passed = positions[:, None] // BLOCK >= doc_ends[None, :]
    return jnp.sum(passed.astype(jnp.int32), axis=1)


def rms_scale(values):
    return values * lax.rsqrt(jnp.mean(values * values, axis=-1, keepdims=True) + NORM_EPS)


def gelu_gate(gate_sum, up_sum):
    return (jax.nn.gelu(gate_sum, approximate=True) * up_sum).astype(jnp.bfloat16)


def attend(query_rows, query_pos, query_doc, key_rows, value_rows, key_pos, key_doc, score_scale):
    scores = (
        lax.dot_general(
            query_rows, key_rows, (((1,), (1,)), ((), ())), preferred_element_type=jnp.float32
        )
        * score_scale
    )
    capped = SOFT_CAP * jnp.tanh(scores / SOFT_CAP)
    visible = (key_pos[None, :] <= query_pos[:, None]) & (key_doc[None, :] == query_doc[:, None])
    weights = jnp.where(visible, jnp.exp(capped), 0.0).astype(jnp.bfloat16)
    numerator = jnp.dot(weights, value_rows, preferred_element_type=jnp.float32)
    denominator = jnp.sum(weights.astype(jnp.float32), axis=1)
    return (numerator, denominator)


def join_halves(own_part, other_part, own_first):
    return jnp.where(
        own_first,
        jnp.concatenate([own_part, other_part], axis=2),
        jnp.concatenate([other_part, own_part], axis=2),
    )


def per_device(
    residual,
    queries,
    key_heads,
    value_heads,
    doc_blocks,
    out_weight,
    post_gain,
    ffn_gain,
    gate_weight,
    up_weight,
):
    tok_rows = queries.shape[0]
    head_size = queries.shape[1]
    score_scale = head_size ** (-0.5)
    query_pos = lax.axis_index("ctx") * tok_rows + jnp.arange(tok_rows, dtype=jnp.int32)
    query_doc = doc_of(query_pos, doc_blocks)
    cosine, sine_value = rope_angles(query_pos, head_size)
    query_rot = rotate(queries, cosine, sine_value, head_size)
    stacked = jnp.stack([key_heads, value_heads])
    own_first = lax.axis_index("tensor") % 2 == 0
    partner = partner_2(stacked, "tensor", 0)
    joined = join_halves(stacked, partner, own_first)
    key_rot = rotate(joined[0], cosine, sine_value, head_size)
    shard_pair = in_one_piece((key_rot, joined[1]), "ctx", 0, 1)
    key_pos = jnp.arange(shard_pair[0].shape[0], dtype=jnp.int32)
    numerator, denominator = attend(
        query_rot,
        query_pos,
        query_doc,
        shard_pair[0],
        shard_pair[1],
        key_pos,
        doc_of(key_pos, doc_blocks),
        score_scale,
    )
    attended = (numerator / denominator[:, None]).astype(jnp.bfloat16)
    attn_rows = sent_and_summed(
        jnp.dot(attended, out_weight, preferred_element_type=jnp.float32).astype(jnp.bfloat16),
        "tensor",
        0,
    )
    mixed_stream = (residual.astype(jnp.float32) + rms_scale(attn_rows) * post_gain).astype(
        jnp.bfloat16
    )
    ffn_input = (rms_scale(mixed_stream.astype(jnp.float32)) * ffn_gain).astype(jnp.bfloat16)
    gathered_rows = collect(ffn_input, "tensor", 0)
    shard_pair = in_one_piece((gate_weight, up_weight), "ctx", 0, 1)
    gate_part = jnp.dot(gathered_rows, shard_pair[0], preferred_element_type=jnp.float32)
    up_part = jnp.dot(gathered_rows, shard_pair[1], preferred_element_type=jnp.float32)
    ffn_hidden = gelu_gate(gate_part, up_part)
    return (mixed_stream, ffn_hidden)


def solution(mesh):
    in_specs = (
        P(("dp", "ctx", "tensor"), None),
        P(("dp", "ctx"), "tensor"),
        P(("dp", "ctx"), "tensor"),
        P(("dp", "ctx"), "tensor"),
        P("dp"),
        P("tensor", None),
        P(),
        P(),
        P("ctx", "tensor"),
        P("ctx", "tensor"),
    )
    out_specs = (P(("dp", "ctx", "tensor"), None), P(("dp", "ctx"), "tensor"))
    return jax.shard_map(
        per_device, mesh=mesh, in_specs=in_specs, out_specs=out_specs, check_vma=False
    )
```

profile of v0, /device:TPU:32, one launch (start us, length us, event | category | flops | bytes accessed | tf_op | source)
XLA Modules:
  0.0 313.3 jit_solution(2621858998864166961)
XLA Ops:
  7.2 0.0 copy-start
  7.2 0.0 copy-start.4
  7.2 0.0 copy-start.3
  7.2 0.0 copy-start.9
  7.2 0.0 all-gather.3.cloned.1.call-start
  7.3 1.0 pad_maximum_fusion.2
  8.3 7.4 %collective-permute-start = (bf16[2,256,128]{2,1,0:T(8,128)(2,1)S(1)}, bf16[2,256,128]{2,1,0:T(8,128)(2,1)S(1)}, u32[]{:S(2)}, u32[]{:S(2)}) collective-permute-start(bf16[2,256,128]{2,1,0:T(8,128)(2,1)S(1)} %pad_maximum_fusion.2), channel_id=1, source_target_pairs={{0,1},{1,0},{2,3},{3,2},{4,5},{5,4},{6,7},{7,6},{8,9},{9,8},{10,11... | collective-permute-start | bytes 393224 | tf_op jit(solution)/shard_map/ppermute | solution.py:17
  15.7 0.9 bitcast_convert_fusion
  16.6 2.0 collective-permute-done
  18.6 1.0 maximum_select_fusion
  19.6 0.6 fusion.48
  20.3 0.7 pad_maximum_fusion.1
  21.0 0.0 all-gather.3.cloned.1.call-update
  21.0 0.0 all-gather.5.cloned.1.call-start
  21.1 0.0 copy-done.4
  21.1 0.0 copy-done.3
  21.1 0.9 pad_maximum_fusion
  22.0 0.0 all-gather.5.cloned.1.call-update
  22.1 0.0 copy-done.9
  22.1 0.2 reduce-window.8
  22.3 0.1 convert_reduce_fusion.3
  22.4 0.1 convert_reduce_fusion.2
  22.5 71.2 %all-gather.3.cloned.1.call-done = bf16[4096,512]{1,0:T(8,128)(2,1)} async-done(((bf16[256,512]{1,0:T(8,128)(2,1)}), bf16[4096,512]{1,0:T(8,128)(2,1)}) %all-gather.3.cloned.1.call-update) | async-done | bytes 4194320 | tf_op jit(solution)/shard_map/all_gather | solution.py:22
  93.7 4.9 %convert_reduce_fusion = (f32[256]{0:T(256)S(1)}, bf16[256,4096]{1,0:T(8,128)(2,1)}) fusion(bf16[4096,512]{1,0:T(8,128)(2,1)} %all-gather.3.cloned.1.call-done, bf16[256,1,128]{2,0,1:T(8,128)(2,1)S(1)} %get-tuple-element.5, bf16[256,1,128]{2,0,1:T(8,128)(2,1)S(1)} %get-tuple-element.4, s32[256]{0:T(256)S(1)} %convert_reduce_fusion.3, ...), kind=kOutput, calls=%fused_computation.11 | convolution fusion | flops 546569984 | bytes 4344832 | tf_op jit(solution)/shard_map/dot_general | solution.py:93
  98.6 0.0 copy-done
  98.6 5.6 %convolution_convert_fusion = bf16[256,3584]{1,0:T(8,128)(2,1)} fusion(bf16[256,3584]{1,0:T(8,128)(2,1)S(1)} %copy-done, bf16[256,4096]{1,0:T(8,128)(2,1)} %get-tuple-element.13, bf16[4096,512]{1,0:T(8,128)(2,1)} %all-gather.3.cloned.1.call-done, f32[256]{0:T(256)S(1)} %get-tuple-element.12), kind=kOutput, calls=%fused_computation.10 | convolution fusion | flops 1007681536 | bytes 7865344 | tf_op jit(solution)/shard_map/dot_general | solution.py:152
  104.2 0.0 copy-start.5
  104.2 0.0 copy-start.7
  104.2 0.0 copy-start.6
  104.2 98.7 %all_to_all.10 = bf16[16,16,3584]{2,1,0:T(8,128)(2,1)S(1)} all-to-all(bf16[16,16,3584]{2,1,0:T(8,128)(2,1)} %bitcast.29), channel_id=1, replica_groups=mesh['dp'=2,'ctx'=16,'tensor'=16] {'tensor'}, dimensions={0} | all-to-all | bytes 3670016 | tf_op jit(solution)/shard_map/all_to_all | solution.py:36
  202.9 0.2 convert_reduce_fusion.1
  203.2 0.1 multiply_reduce_fusion
  203.3 0.0 copy-done.5
  203.3 0.0 copy-done.7
  203.3 0.2 fusion.36
  203.6 0.0 copy-start.2
  203.6 0.0 copy-done.6
  203.6 0.1 fusion.38
  203.7 0.2 broadcast_in_dim.6
  203.9 92.2 %all_to_all.11 = bf16[16,16,3584]{2,1,0:T(8,128)(2,1)} all-to-all(bf16[16,16,3584]{2,1,0:T(8,128)(2,1)S(1)} %broadcast_in_dim.6), channel_id=1, replica_groups=mesh['dp'=2,'ctx'=16,'tensor'=16] {'tensor'}, dimensions={0} | all-to-all | bytes 3670016 | tf_op jit(solution)/shard_map/all_to_all | solution.py:48
  296.0 0.0 all-gather.5.cloned.1.call-done
  296.0 0.0 copy-start.1
  296.0 0.0 copy-start.8
  296.0 5.7 %fusion.33 = f32[256,896]{1,0:T(8,128)S(1)} fusion(bf16[256,3584]{1,0:T(8,128)(2,1)} %bitcast.27, bf16[3584,1792]{1,0:T(8,128)(2,1)} %all-gather.5.cloned.1.call-done), kind=kOutput, calls=%fused_computation.29 | convolution fusion | flops 1646002176 | bytes 9175040 | tf_op jit(solution)/shard_map/dot_general | solution.py:162
  301.7 0.0 copy-done.2
  301.7 0.0 copy-done.1
  301.7 1.9 copy-done.8
  303.6 2.8 fusion.16
  (8 shorter events, 0.1 us)
Async XLA Ops:
  7.2 91.4 %copy-start = (bf16[256,3584]{1,0:T(8,128)(2,1)S(1)}, bf16[256,3584]{1,0:T(8,128)(2,1)}, u32[]{:S(2)}) copy-start(bf16[256,3584]{1,0:T(8,128)(2,1)} %param.15) | copy-start | bytes 5505028
  7.2 13.9 %copy-start.4 = (bf16[224,896]{1,0:T(8,128)(2,1)S(1)}, bf16[224,896]{1,0:T(8,128)(2,1)}, u32[]{:S(2)}) copy-start(bf16[224,896]{1,0:T(8,128)(2,1)} %param.18) | copy-start | bytes 1204228
  7.2 13.9 %copy-start.3 = (bf16[224,896]{1,0:T(8,128)(2,1)S(1)}, bf16[224,896]{1,0:T(8,128)(2,1)}, u32[]{:S(2)}) copy-start(bf16[224,896]{1,0:T(8,128)(2,1)} %param.19) | copy-start | bytes 1204228
  7.2 14.9 %copy-start.9 = (s32[6]{0:T(128)S(1)}, s32[6]{0:T(128)}, u32[]{:S(2)}) copy-start(s32[6]{0:T(128)} %param.14) | copy-start | bytes 76
  7.2 86.5 %all-gather.3.cloned.1.call-start = ((), (), s32[]{:S(2)}) async-start(), calls=%async_computation.2 | async-start | bytes 4456448 | tf_op jit(solution)/shard_map/all_gather | solution.py:22
  8.3 10.3 %collective-permute-start = (bf16[2,256,128]{2,1,0:T(8,128)(2,1)S(1)}, bf16[2,256,128]{2,1,0:T(8,128)(2,1)S(1)}, u32[]{:S(2)}, u32[]{:S(2)}) collective-permute-start(bf16[2,256,128]{2,1,0:T(8,128)(2,1)S(1)} %pad_maximum_fusion.2), channel_id=1, source_target_pairs={{0,1},{1,0},{2,3},{3,2},{4,5},{5,4},{6,7},{7,6},{8,9},{9,8},{10,11... | collective-permute-start | bytes 393224 | tf_op jit(solution)/shard_map/ppermute | solution.py:17
  21.0 275.0 %all-gather.5.cloned.1.call-start = ((), (), s32[]{:S(2)}) async-start(), calls=%async_computation.3 | async-start | bytes 13647872 | tf_op jit(solution)/shard_map/all_gather | solution.py:22
  104.2 99.1 %copy-start.5 = (bf16[16,3584]{1,0:T(8,128)(2,1)S(1)}, bf16[16,3584]{1,0:T(8,128)(2,1)}, u32[]{:S(2)}) copy-start(bf16[16,3584]{1,0:T(8,128)(2,1)} %param.10) | copy-start | bytes 344068
  104.2 99.1 %copy-start.7 = (f32[3584]{0:T(1024)S(1)}, f32[3584]{0:T(1024)}, u32[]{:S(2)}) copy-start(f32[3584]{0:T(1024)} %param.16) | copy-start | bytes 43012
  104.2 99.4 %copy-start.6 = (f32[3584]{0:T(1024)S(1)}, f32[3584]{0:T(1024)}, u32[]{:S(2)}) copy-start(f32[3584]{0:T(1024)} %param.17) | copy-start | bytes 43012
  203.6 98.2 %copy-start.2 = (bf16[16,3584]{1,0:T(8,128)(2,1)}, bf16[16,3584]{1,0:T(8,128)(2,1)S(1)}, u32[]{:S(2)}) copy-start(bf16[16,3584]{1,0:T(8,128)(2,1)S(1)} %get-tuple-element.3) | copy-start | bytes 344068
  296.0 5.7 %copy-start.1 = (bf16[16,16,3584]{2,1,0:T(8,128)(2,1)S(1)}, bf16[16,16,3584]{2,1,0:T(8,128)(2,1)}, u32[]{:S(2)}) copy-start(bf16[16,16,3584]{2,1,0:T(8,128)(2,1)} %all_to_all.11) | copy-start | bytes 5505028
  296.0 7.6 %copy-start.8 = (bf16[3584,1792]{1,0:T(8,128)(2,1)S(1)}, bf16[3584,1792]{1,0:T(8,128)(2,1)}, u32[]{:S(2)}) copy-start(bf16[3584,1792]{1,0:T(8,128)(2,1)} %all-gather.5.cloned.1.call-done) | copy-start | bytes 38535172
Sparse Core Ops, SparseCore 0:
  21.1 72.5 all-gather.2
  97.0 105.8 all-gather.4
where the time goes:
time: 314 us; the launch traced here: 313 us
  blocking collectives  191 us (61%)
  waiting for transfers between devices  73.2 us (23%)
  matrix products  19 us (6%)
  between operations  14.2 us (5%)
  starting transfers between devices  7.44 us (2%)
  other arithmetic  6.43 us (2%)
    all_to_all x1, blocking collectives, sent_and_summed(): blocks = lax.all_to_all(split_up(array, dim, peers), axis, 0, 0, tiled=True)  98.7 us
    all_to_all x1, blocking collectives, sent_to_all(): lax.all_to_all(jnp.broadcast_to(array[None], (peers, *array.shape)), axis...  92.2 us
    all_gather x2, waiting for transfers between devices, in_one_piece(): out, at, done = (lax.all_gather(both, axis, axis=dim, tiled=True), 0, [])  71.2 us
    ppermute x1, starting transfers between devices, partner_2(): return lax.ppermute(value, axis, pairs)  7.36 us
  transfers between devices with their start and end apart: 3, of which 2 were waited for; matrix products, arithmetic and copies ran while one was open for 4% of the time, Pallas kernels for 0%

commit v1 on v0

v1 whole, which is shorter than its diff:
```python
import functools

import jax
import jax.numpy as jnp
import numpy as np
from jax import lax
from jax.experimental import pallas as pl
from jax.experimental.pallas import tpu as pltpu
from jax.sharding import PartitionSpec as P

MESH = pl.DeviceIdType.MESH
BLOCK = 32
SOFT_CAP = 50.0
NORM_EPS = 1e-06
ROPE_BASE = 10000.0
RING = 16
TOK = 256
HEAD = 256
HALF = 128
WIDTH = 3584
ROWS = 16
SUBS = 4
SUB = WIDTH // SUBS
F32 = jnp.float32
BF16 = jnp.bfloat16


def rope_tables():
    freq = ROPE_BASE ** (-(np.arange(HALF, dtype=np.float64) * 2.0) / HEAD)
    inner = np.arange(TOK, dtype=np.float64)[:, None] * freq[None, :]
    outer = (np.arange(16, dtype=np.float64) * TOK)[:, None] * freq[None, :]
    return tuple(np.asarray(f(a), np.float32) for a in (inner, outer) for f in (np.cos, np.sin))


class Sends:
    def __init__(self):
        self.pending = []

    def go(self, copy, cond=None):
        if cond is None:
            copy.start()
        else:
            pl.when(cond)(copy.start)
        self.pending.append((copy, cond))

    def drain(self):
        for copy, cond in self.pending:
            if cond is None:
                copy.wait_send()
            else:
                pl.when(cond)(copy.wait_send)
        self.pending = []


def layer_kernel(
    q_ref,
    k_ref,
    v_ref,
    doc_ref,
    res_ref,
    post_ref,
    ffn_ref,
    cos_in,
    sin_in,
    cos_out,
    sin_out,
    ow_hbm,
    mixed_ref,
    x_out,
    ow,
    rawk,
    kk,
    vv,
    qrot,
    num,
    den,
    term,
    rs_r,
    rs_l,
    acc,
    x_buf,
    ow_sem,
    pair_send,
    pair_recv,
    kv_send,
    k_recv,
    v_recv,
    rs_send,
    rs_recv,
    ag_send,
    ag_recv,
):
    dp = lax.axis_index("dp")
    c = lax.axis_index("ctx")
    t = lax.axis_index("tensor")
    row = c // 8
    x = (c % 8) // 2
    core = c % 2
    par = t % 2

    def at(r, xx, kk_, d=dp):
        return (d, r * 8 + xx * 2 + kk_, t)

    x_up = (x + 1) % 4
    x_dn = (x + 3) % 4
    right_x = at(row, x_up, core)
    left_x = at(row, x_dn, core)
    cross = at(1 - row, x, core)
    sib = at(row, x, 1 - core)
    z_up = (dp, c, (t + 1) % RING)
    z_dn = (dp, c, (t + RING - 1) % RING)
    mate = (dp, c, t + 1 - 2 * par)

    barrier = pltpu.get_barrier_semaphore()
    friends = (right_x, left_x, cross, sib, z_up, z_dn)
    for friend in friends:
        pl.semaphore_signal(barrier, inc=1, device_id=friend, device_id_type=MESH)
    ow_copy = pltpu.make_async_copy(ow_hbm, ow, ow_sem)
    ow_copy.start()

    sends = Sends()

    def remote(src, dst, send, recv, to):
        return pltpu.make_async_remote_copy(
            src_ref=src, dst_ref=dst, send_sem=send, recv_sem=recv, device_id=to, device_id_type=MESH
        )

    own_lanes = pl.ds(pl.multiple_of(par * HALF, HALF), HALF)
    pl.semaphore_wait(barrier, len(friends))
    pair_k = remote(k_ref, rawk.at[par], pair_send.at[0], pair_recv.at[0], mate)
    pair_v = remote(v_ref, vv.at[c, :, own_lanes], pair_send.at[1], pair_recv.at[1], mate)
    sends.go(pair_k)
    sends.go(pair_v)

    cb = cos_out[pl.ds(c, 1), :]
    sb = sin_out[pl.ds(c, 1), :]
    cosine = cos_in[...] * cb - sin_in[...] * sb
    sine = sin_in[...] * cb + cos_in[...] * sb

    def turned(a, b, where):
        a, b = a.astype(F32), b.astype(F32)
        where[:, :HALF] = (a * cosine - b * sine).astype(BF16)
        where[:, HALF:] = (b * cosine + a * sine).astype(BF16)

    turned(q_ref[:, :HALF], q_ref[:, HALF:], qrot)
    rawk[par] = k_ref[...]
    vv[c, :, own_lanes] = v_ref[...]
    num[...] = jnp.zeros_like(num)
    den[...] = jnp.zeros_like(den)

    qpos = c * TOK + lax.broadcasted_iota(jnp.int32, (TOK, 1), 0)
    begin = jnp.zeros((TOK, 1), jnp.int32)
    total = 0
    for e in range(5):
        total = total + doc_ref[e]
        edge = total * BLOCK
        begin = jnp.where(qpos >= edge, jnp.maximum(begin, edge), begin)

    def attend(b):
        lane = b * TOK + lax.broadcasted_iota(jnp.int32, (1, TOK), 1)
        scores = lax.dot_general(
            qrot[...], kk[b], (((1,), (1,)), ((), ())), preferred_element_type=F32
        )
        capped = jnp.tanh(scores * (1.0 / (SOFT_CAP * HEAD**0.5))) * (SOFT_CAP / np.log(2.0))
        visible = (lane >= begin) & (lane <= qpos)
        weights = jnp.where(visible, jnp.exp2(capped), 0.0).astype(BF16)
        wide = weights.astype(F32)
        den[...] += wide[:, :HALF] + wide[:, HALF:]
        num[...] += jnp.dot(weights, vv[b], preferred_element_type=F32)

    slot = iter(range(64))

    def k_copy(b, to):
        return remote(kk.at[b], kk.at[b], kv_send.at[next(slot)], k_recv.at[b], to)

    def v_copy(b, to):
        return remote(vv.at[b], vv.at[b], kv_send.at[next(slot)], v_recv.at[b], to)

    def k_wait(b, cond):
        got = remote(kk.at[b], kk.at[b], kv_send.at[0], k_recv.at[b], sib)
        pl.when(cond)(got.wait_recv)

    def v_wait(b, cond):
        got = remote(vv.at[b], vv.at[b], kv_send.at[0], v_recv.at[b], sib)
        pl.when(cond)(got.wait_recv)

    pair_k.wait_recv()
    turned(rawk[0], rawk[1], kk.at[c])

    def spread(copy):
        sends.go(copy(c, right_x), x < 3)
        sends.go(copy(c, left_x), x == 0)
        sends.go(copy(c, cross), row == 0)
        sends.go(copy(c, sib), core == 0)

    spread(k_copy)
    pair_v.wait_recv()
    spread(v_copy)
    attend(c)

    mid = (x == 1) | (x == 2)
    lower = row == 1
    for hop in (1, 2, 3):
        b = jnp.maximum(c - 2 * hop, 0)
        here = x >= hop
        for wait, copy in ((k_wait, k_copy), (v_wait, v_copy)):
            wait(b, here)
            if hop == 1:
                sends.go(copy(b, right_x), mid)
            sends.go(copy(b, sib), here)
        if hop == 1:
            own0 = jnp.maximum(c - 8, 0)
            for wait, copy in ((k_wait, k_copy), (v_wait, v_copy)):
                wait(own0, lower)
                sends.go(copy(own0, left_x), lower & (x > 0))
                sends.go(copy(own0, right_x), lower & (x == 3))
                sends.go(copy(own0, sib), lower & (core == 1))
    for hop in (1, 2, 3):
        b = jnp.clip(c - 8 + 2 * hop, 0, 15)
        here = lower & (x + hop <= 3)
        for wait, copy in ((k_wait, k_copy), (v_wait, v_copy)):
            wait(b, here)
            if hop == 1:
                sends.go(copy(b, left_x), lower & mid)
            sends.go(copy(b, sib), here)

    first = jnp.maximum(c - 8, 0)

    def visit(b, carry):
        other = (b % 2) != core
        k_wait(b, other)
        v_wait(b, other)
        attend(b)
        return carry

    lax.fori_loop(first, c, visit, 0)
    ow_copy.wait()

    sums = jnp.sum(den[...], axis=1, keepdims=True)
    attended = (num[...] / sums).astype(BF16)

    def lanes(s):
        return pl.ds(s * SUB, SUB)

    def block(d):
        return pl.ds(pl.multiple_of(lax.rem(t + d + RING, RING) * ROWS, ROWS), ROWS)

    HOPS = RING // 2
    flows = (
        (0, rs_r, z_up, 1, (0, 1)),
        (1, rs_l, z_dn, -1, (2, 3)),
    )

    def rs_step(k, s):
        for f, buf, to, sign, early in flows:
            begin_at = 1 if s in early else 2
            if k < begin_at:
                continue
            away = sign * (HOPS + 1 - k)
            if k == begin_at:
                src = term.at[block(away), lanes(s)]
            else:
                src = buf.at[k - 2, :, lanes(s)]
                remote(src, src, rs_send.at[f, k - 2, s], rs_recv.at[f, k - 2, s], to).wait_recv()
                buf[k - 2, :, lanes(s)] = (
                    buf[k - 2, :, lanes(s)].astype(F32) + term[block(away), lanes(s)].astype(F32)
                ).astype(BF16)
            sends.go(
                remote(src, buf.at[k - 1, :, lanes(s)], rs_send.at[f, k - 1, s], rs_recv.at[f, k - 1, s], to)
            )

    for s in range(SUBS):
        term[:, lanes(s)] = jnp.dot(attended, ow[:, lanes(s)], preferred_element_type=F32).astype(BF16)
        rs_step(1, s)
    for k in range(2, HOPS + 1):
        for s in range(SUBS):
            rs_step(k, s)

    square = jnp.zeros((ROWS, 1), F32)
    for s in range(SUBS):
        for f, buf, to, _, _ in flows:
            src = buf.at[HOPS - 1, :, lanes(s)]
            remote(src, src, rs_send.at[f, HOPS - 1, s], rs_recv.at[f, HOPS - 1, s], to).wait_recv()
        part = (
            term[block(0), lanes(s)].astype(F32)
            + rs_r[HOPS - 1, :, lanes(s)].astype(F32)
            + rs_l[HOPS - 1, :, lanes(s)].astype(F32)
        )
        acc[:, lanes(s)] = part
        square += jnp.sum(part * part, axis=1, keepdims=True)
    scale = lax.rsqrt(square / WIDTH + NORM_EPS)
    mixed = (res_ref[...].astype(F32) + acc[...] * scale * post_ref[...]).astype(BF16)
    mixed_ref[...] = mixed
    wide = mixed.astype(F32)
    scale = lax.rsqrt(jnp.sum(wide * wide, axis=1, keepdims=True) / WIDTH + NORM_EPS)
    x_buf[block(0), :] = (wide * scale * ffn_ref[...]).astype(BF16)

    ag_flows = ((0, z_up, -1, (0, 1)), (1, z_dn, 1, (2, 3)))

    def ag_got(k, s):
        for f, to, sign, late in ag_flows:
            if k == HOPS and s not in late:
                continue
            src = x_buf.at[block(sign * k), lanes(s)]
            remote(src, src, ag_send.at[f, k - 1, s], ag_recv.at[f, k - 1, s], to).wait_recv()

    for k in range(1, HOPS + 1):
        for s in range(SUBS):
            for f, to, sign, late in ag_flows:
                if k > 1:
                    got = x_buf.at[block(sign * (k - 1)), lanes(s)]
                    remote(got, got, ag_send.at[f, k - 2, s], ag_recv.at[f, k - 2, s], to).wait_recv()
                if k == HOPS and s not in late:
                    continue
                src = x_buf.at[block(sign * (k - 1)), lanes(s)]
                sends.go(remote(src, src, ag_send.at[f, k - 1, s], ag_recv.at[f, k - 1, s], to))
    for s in range(SUBS):
        ag_got(HOPS, s)
    x_out[...] = x_buf[...]
    sends.drain()


def attention_half(q, k, v, doc_blocks, residual, post_gain, ffn_gain, out_weight):
    vmem = pl.BlockSpec(memory_space=pltpu.VMEM)
    tables = [jnp.asarray(a) for a in rope_tables()]
    half = RING // 2
    dma = pltpu.SemaphoreType.DMA
    return pl.pallas_call(
        layer_kernel,
        out_shape=(
            jax.ShapeDtypeStruct((ROWS, WIDTH), BF16),
            jax.ShapeDtypeStruct((TOK, WIDTH), BF16),
        ),
        in_specs=[vmem] * 3
        + [pl.BlockSpec(memory_space=pltpu.SMEM)]
        + [vmem] * 7
        + [pl.BlockSpec(memory_space=pl.ANY)],
        out_specs=(vmem, vmem),
        scratch_shapes=[
            pltpu.VMEM((HEAD, WIDTH), BF16),
            pltpu.VMEM((2, TOK, HALF), BF16),
            pltpu.VMEM((16, TOK, HEAD), BF16),
            pltpu.VMEM((16, TOK, HEAD), BF16),
            pltpu.VMEM((TOK, HEAD), BF16),
            pltpu.VMEM((TOK, HEAD), F32),
            pltpu.VMEM((TOK, HALF), F32),
            pltpu.VMEM((TOK, WIDTH), BF16),
            pltpu.VMEM((half, ROWS, WIDTH), BF16),
            pltpu.VMEM((half, ROWS, WIDTH), BF16),
            pltpu.VMEM((ROWS, WIDTH), F32),
            pltpu.VMEM((TOK, WIDTH), BF16),
            dma,
            dma((2,)),
            dma((2,)),
            dma((40,)),
            dma((16,)),
            dma((16,)),
            dma((2, half, SUBS)),
            dma((2, half, SUBS)),
            dma((2, half, SUBS)),
            dma((2, half, SUBS)),
        ],
        compiler_params=pltpu.CompilerParams(
            collective_id=0, has_side_effects=True, vmem_limit_bytes=48 * 1024 * 1024
        ),
        cost_estimate=pl.CostEstimate(flops=2_000_000_000, bytes_accessed=8_000_000, transcendentals=0),
    )(
        q,
        k,
        v,
        doc_blocks,
        residual,
        post_gain.reshape(1, WIDTH),
        ffn_gain.reshape(1, WIDTH),
        *tables,
        out_weight,
    )


def gelu_gate(gate_sum, up_sum):
    return (jax.nn.gelu(gate_sum, approximate=True) * up_sum).astype(BF16)


def per_device(
    residual,
    queries,
    key_heads,
    value_heads,
    doc_blocks,
    out_weight,
    post_gain,
    ffn_gain,
    gate_weight,
    up_weight,
):
    both = jnp.concatenate([gate_weight, up_weight], axis=1)
    whole = lax.all_gather(both, "ctx", axis=0, tiled=True)
    mixed_stream, rows = attention_half(
        queries, key_heads, value_heads, doc_blocks, residual, post_gain, ffn_gain, out_weight
    )
    columns = gate_weight.shape[1]
    gate_part = jnp.dot(rows, whole[:, :columns], preferred_element_type=F32)
    up_part = jnp.dot(rows, whole[:, columns:], preferred_element_type=F32)
    return (mixed_stream, gelu_gate(gate_part, up_part))


def solution(mesh):
    in_specs = (
        P(("dp", "ctx", "tensor"), None),
        P(("dp", "ctx"), "tensor"),
        P(("dp", "ctx"), "tensor"),
        P(("dp", "ctx"), "tensor"),
        P("dp"),
        P("tensor", None),
        P(),
        P(),
        P("ctx", "tensor"),
        P("ctx", "tensor"),
    )
    out_specs = (P(("dp", "ctx", "tensor"), None), P(("dp", "ctx"), "tensor"))
    return jax.shard_map(
        per_device, mesh=mesh, in_specs=in_specs, out_specs=out_specs, check_vma=False
    )
```

time: 314 us -> 143 us (0.46)
  the two profiles are of different devices: /device:TPU:32 before, /device:TPU:1 now
where the time goes in v1:
time: 143 us
  Pallas kernels  71 us (50%)
  waiting for transfers between devices  39.8 us (28%)
  between operations  14.2 us (10%)
  matrix products  8.52 us (6%)
  local copies, waits for them, and re-layouts  6.66 us (5%)
  other arithmetic  2.24 us (2%)
    pallas_call x1, Pallas kernels, attention_half(): pl.pallas_call(layer_kernel, out_shape=(jax.ShapeDtypeStruct((ROWS, WIDTH...  71 us
    all_gather x1, waiting for transfers between devices, per_device(): whole = lax.all_gather(both, 'ctx', axis=0, tiled=True)  39.8 us
    dot_general x1, matrix products, per_device(): gate_part = jnp.dot(rows, whole[:, :columns], preferred_element_type=F32)  5.68 us
    unnamed x27, local copies, waits for them, and re-layouts  5.19 us
  transfers between devices with their start and end apart: 1, of which 1 were waited for; matrix products, arithmetic and copies ran while one was open for 1% of the time, Pallas kernels for 50%

profile of v1, /device:TPU:1, one launch (start us, length us, event | category | flops | bytes accessed | tf_op | source)
XLA Modules:
  0.0 142.5 jit_solution(7613903151731014097)
XLA Ops:
  7.2 0.0 copy-start.6
  7.2 0.0 copy-start.7
  7.2 0.0 copy-start
  7.2 0.0 copy-start.5
  7.2 0.0 copy-start.4
  7.2 0.0 copy-start.3
  7.2 0.0 copy-start.1
  7.2 0.0 copy-start.2
  7.3 0.0 all-gather.2.cloned.1.call-start
  7.3 2.2 %pad_maximum_fusion = bf16[224,1792]{1,0:T(8,128)(2,1)} fusion(bf16[224,896]{1,0:T(8,128)(2,1)} %param.23, bf16[224,896]{1,0:T(8,128)(2,1)} %param.22), kind=kLoop, calls=%fused_computation.14 | loop fusion | flops 1605632 | bytes 1605632 | tf_op jit(solution)/shard_map/concatenate | solution.py:396
  9.5 0.0 all-gather.2.cloned.1.call-update
  9.6 0.7 reshape.10.post_ref
  10.3 0.7 reshape.11.ffn_ref
  11.0 0.0 copy-done.6
  11.0 0.0 copy-done.7
  11.0 0.0 copy-done
  11.1 0.0 copy-done.5
  11.1 0.0 copy-done.4
  11.1 0.0 copy-done.3
  11.1 0.0 copy-done.1
  11.1 0.0 copy-done.2
  11.1 0.0 copy-start.8
  11.1 0.7 copy-done.8
  11.8 0.0 copy-start.9
  11.8 0.7 copy-done.9
  12.5 71.0 %shard_map.149 = (bf16[16,3584]{1,0:T(8,128)(2,1)S(1)}, bf16[256,3584]{1,0:T(8,128)(2,1)S(1)}) custom-call(bf16[256,256]{1,0:T(8,128)(2,1)S(1)} %copy-done.1, bf16[256,128]{1,0:T(8,128)(2,1)S(1)} %copy-done.3, bf16[256,128]{1,0:T(8,128)(2,1)S(1)} %copy-done.4, s32[6]{0:T(128)S(1)} %copy-done.5, bf16[16,3584]{1,0:T(8,128)(2,1)S(1)} %copy-done.2, ...), custom_call_target="tpu_custom_call" | custom-call | flops 2000000000 | bytes 8000000 | tf_op jit(solution)/shard_map/pallas_call | solution.py:328
  83.6 0.0 copy-start.10
  83.6 1.2 copy-done.10
  84.8 39.8 %all-gather.2.cloned.1.call-done = bf16[3584,1792]{1,0:T(8,128)(2,1)} async-done(((bf16[224,1792]{1,0:T(8,128)(2,1)}), bf16[3584,1792]{1,0:T(8,128)(2,1)}) %all-gather.2.cloned.1.call-update) | async-done | bytes 12845072 | tf_op jit(solution)/shard_map/all_gather | solution.py:397
  124.6 0.0 copy-start.11
  124.6 0.0 copy-start.12
  124.6 5.7 %fusion.16 = f32[256,896]{1,0:T(8,128)S(1)} fusion(bf16[256,3584]{1,0:T(8,128)(2,1)} %copy-done.10, bf16[3584,1792]{1,0:T(8,128)(2,1)} %all-gather.2.cloned.1.call-done), kind=kOutput, calls=%fused_computation.13 | convolution fusion | flops 1646002176 | bytes 9175040 | tf_op jit(solution)/shard_map/dot_general | solution.py:402
  130.3 0.0 copy-done.11
  130.3 1.9 %copy-done.12 = bf16[3584,1792]{1,0:T(8,128)(2,1)S(1)} copy-done((bf16[3584,1792]{1,0:T(8,128)(2,1)S(1)}, bf16[3584,1792]{1,0:T(8,128)(2,1)}, u32[]{:S(2)}) %copy-start.12) | copy-done | bytes 12845080
  132.2 2.8 %fusion.7 = bf16[256,896]{1,0:T(8,128)(2,1)} fusion(f32[256,896]{1,0:T(8,128)S(1)} %fusion.16, bf16[256,3584]{1,0:T(8,128)(2,1)S(1)} %copy-done.11, bf16[3584,1792]{1,0:T(8,128)(2,1)S(1)} %copy-done.12), kind=kOutput, calls=%fused_computation.6 | convolution fusion | flops 1644625920 | bytes 9633792 | tf_op jit(solution)/shard_map/dot_general | solution.py:403
  135.0 0.6 copy.17
Async XLA Ops:
  7.2 3.9 %copy-start.6 = (f32[256,128]{1,0:T(8,128)S(1)}, f32[256,128]{1,0:T(8,128)}, u32[]{:S(2)}) copy-start(f32[256,128]{1,0:T(8,128)} %constant.17.clone.sin_in) | copy-start | bytes 393220
  7.2 3.9 %copy-start.7 = (f32[256,128]{1,0:T(8,128)S(1)}, f32[256,128]{1,0:T(8,128)}, u32[]{:S(2)}) copy-start(f32[256,128]{1,0:T(8,128)} %constant.16.clone.cos_in) | copy-start | bytes 393220
  7.2 3.9 %copy-start = (bf16[256,3584]{1,0:T(8,128)(2,1)S(1)}, bf16[256,3584]{1,0:T(8,128)(2,1)}, u32[]{:S(2)}) copy-start(bf16[256,3584]{1,0:T(8,128)(2,1)} %ow_hbm.1) | copy-start | bytes 5505028
  7.2 3.9 %copy-start.5 = (s32[6]{0:T(128)S(1)}, s32[6]{0:T(128)}, u32[]{:S(2)}) copy-start(s32[6]{0:T(128)} %doc_ref.1) | copy-start | bytes 76
  7.2 3.9 %copy-start.4 = (bf16[256,128]{1,0:T(8,128)(2,1)S(1)}, bf16[256,128]{1,0:T(8,128)(2,1)}, u32[]{:S(2)}) copy-start(bf16[256,128]{1,0:T(8,128)(2,1)} %v_ref.1) | copy-start | bytes 196612
  7.2 3.9 %copy-start.3 = (bf16[256,128]{1,0:T(8,128)(2,1)S(1)}, bf16[256,128]{1,0:T(8,128)(2,1)}, u32[]{:S(2)}) copy-start(bf16[256,128]{1,0:T(8,128)(2,1)} %k_ref.1) | copy-start | bytes 196612
  7.2 3.9 %copy-start.1 = (bf16[256,256]{1,0:T(8,128)(2,1)S(1)}, bf16[256,256]{1,0:T(8,128)(2,1)}, u32[]{:S(2)}) copy-start(bf16[256,256]{1,0:T(8,128)(2,1)} %q_ref.1) | copy-start | bytes 393220
  7.2 3.9 %copy-start.2 = (bf16[16,3584]{1,0:T(8,128)(2,1)S(1)}, bf16[16,3584]{1,0:T(8,128)(2,1)}, u32[]{:S(2)}) copy-start(bf16[16,3584]{1,0:T(8,128)(2,1)} %res_ref.1) | copy-start | bytes 344068
  7.3 117.4 %all-gather.2.cloned.1.call-start = ((), (), s32[]{:S(2)}) async-start(), calls=%async_computation | async-start | bytes 13647872 | tf_op jit(solution)/shard_map/all_gather | solution.py:397
  11.1 0.7 copy-start.8
  11.8 0.7 copy-start.9
  83.6 1.2 copy-start.10
  124.6 5.7 %copy-start.11 = (bf16[256,3584]{1,0:T(8,128)(2,1)S(1)}, bf16[256,3584]{1,0:T(8,128)(2,1)}, u32[]{:S(2)}) copy-start(bf16[256,3584]{1,0:T(8,128)(2,1)} %copy-done.10) | copy-start | bytes 5505028
  124.6 7.6 %copy-start.12 = (bf16[3584,1792]{1,0:T(8,128)(2,1)S(1)}, bf16[3584,1792]{1,0:T(8,128)(2,1)}, u32[]{:S(2)}) copy-start(bf16[3584,1792]{1,0:T(8,128)(2,1)} %all-gather.2.cloned.1.call-done) | copy-start | bytes 38535172
Sparse Core Ops, SparseCore 0:
  11.4 113.1 all-gather.1

commit v2 on v1

--- a/solution.py
+++ b/solution.py
@@ -21,6 +21,13 @@
 ROWS = 16
 SUBS = 4
 SUB = WIDTH // SUBS
+SHARD = 224
+COLS = 896
+TILES = COLS // 128
+MAIN = 144
+REST = SHARD - MAIN
+NEAR = 80
+FAR = MAIN - NEAR
 F32 = jnp.float32
 BF16 = jnp.bfloat16
 
@@ -65,9 +72,12 @@
     cos_out,
     sin_out,
     ow_hbm,
+    gate_hbm,
+    up_hbm,
     mixed_ref,
-    x_out,
+    hidden_ref,
     ow,
+    w,
     rawk,
     kk,
     vv,
@@ -89,6 +99,9 @@
     rs_recv,
     ag_send,
     ag_recv,
+    w_load,
+    w_send,
+    w_recv,
 ):
     dp = lax.axis_index("dp")
     c = lax.axis_index("ctx")
@@ -110,13 +123,28 @@
     z_up = (dp, c, (t + 1) % RING)
     z_dn = (dp, c, (t + RING - 1) % RING)
     mate = (dp, c, t + 1 - 2 * par)
+    twin = at(row, x, core, 1 - dp)
+    other = at(1 - row, x, core, 1 - dp)
 
     barrier = pltpu.get_barrier_semaphore()
-    friends = (right_x, left_x, cross, sib, z_up, z_dn)
+    friends = (right_x, left_x, cross, sib, z_up, z_dn, twin, other)
     for friend in friends:
         pl.semaphore_signal(barrier, inc=1, device_id=friend, device_id_type=MESH)
     ow_copy = pltpu.make_async_copy(ow_hbm, ow, ow_sem)
     ow_copy.start()
+    own_rows = pl.ds(pl.multiple_of(c * SHARD, 16), SHARD)
+    loads = []
+    for n in range(TILES):
+        for i, ref in enumerate((gate_hbm, up_hbm)):
+            loads.append(
+                pltpu.make_async_copy(
+                    ref.at[:, pl.ds(n * 128, 128)],
+                    w.at[own_rows, pl.ds(n * 256 + i * 128, 128)],
+                    w_load.at[n, i],
+                )
+            )
+    for load in loads:
+        load.start()
 
     sends = Sends()
 
@@ -224,6 +252,80 @@
                 sends.go(copy(b, left_x), lower & mid)
             sends.go(copy(b, sib), here)
 
+    w_slot = iter(range(64))
+
+    def shard(r, dx, plane=core):
+        return r * 8 + ((x + dx) % 4) * 2 + plane
+
+    def cut(b, start, size):
+        return w.at[pl.ds(pl.multiple_of(b * SHARD + start, 16), size), :]
+
+    def w_go(b, start, size, kind, to):
+        ref = cut(b, start, size)
+        sends.go(remote(ref, ref, w_send.at[next(w_slot)], w_recv.at[b, kind], to))
+
+    def w_wait(b, size, kind):
+        ref = cut(b, 0, size)
+        remote(ref, ref, w_send.at[0], w_recv.at[b, kind], sib).wait_recv()
+
+    main_at = REST * dp
+    rest_at = MAIN * dp
+    twin_main_at = REST * (1 - dp)
+    twin_rest_at = MAIN * (1 - dp)
+
+    def w_first():
+        for load in loads:
+            load.wait()
+        b = shard(row, 0)
+        w_go(b, twin_main_at, MAIN, 0, other)
+        w_go(b, main_at, MAIN, 0, right_x)
+        w_go(b, main_at, MAIN, 0, left_x)
+        w_go(b, rest_at, REST, 1, other)
+        w_go(b, 0, SHARD, 0, sib)
+
+    def w_cross():
+        b = shard(1 - row, 0)
+        w_wait(b, MAIN, 0)
+        w_go(b, main_at, MAIN, 0, right_x)
+        w_go(b, main_at, MAIN, 0, left_x)
+        w_go(b, main_at, MAIN, 0, sib)
+
+    def w_cross_rest():
+        b = shard(1 - row, 0)
+        w_wait(b, REST, 1)
+        w_go(b, twin_rest_at, REST, 1, sib)
+
+    def w_next(r):
+        for dx, to, start, size, kind in ((-1, right_x, 0, NEAR, 0), (1, left_x, NEAR, FAR, 2)):
+            b = shard(r, dx)
+            w_wait(b, MAIN, 0)
+            w_go(b, main_at + start, size, kind, to)
+            w_go(b, rest_at, REST, 1, at((row + r) % 2, x, core, 1 - dp))
+            w_go(b, main_at, MAIN, 0, sib)
+
+    def w_far(r):
+        b = shard(r, 2)
+        w_wait(b, NEAR, 0)
+        w_wait(b, FAR, 2)
+        w_go(b, rest_at, REST, 1, twin)
+        w_go(b, main_at, MAIN, 0, sib)
+
+    def w_rest(r, dx):
+        b = shard(r, dx)
+        w_wait(b, REST, 1)
+        w_go(b, twin_rest_at, REST, 1, sib)
+
+    def w_last():
+        for r in (row, 1 - row):
+            for dx in (0, -1, 1, 2):
+                b = shard(r, dx, 1 - core)
+                if dx == 0 and r is row:
+                    w_wait(b, SHARD, 0)
+                else:
+                    w_wait(b, MAIN, 0)
+                    w_wait(b, REST, 1)
+
+    w_first()
     first = jnp.maximum(c - 8, 0)
 
     def visit(b, carry):
@@ -275,6 +377,17 @@
     for k in range(2, HOPS + 1):
         for s in range(SUBS):
             rs_step(k, s)
+        if k == 4:
+            w_next(row)
+        if k == 5:
+            w_cross()
+        if k == 6:
+            w_far(row)
+        if k == 7:
+            w_cross_rest()
+
+    def whole_row(ref):
+        return jnp.concatenate([ref[i : i + 1, :] for i in range(WIDTH // 128)], axis=1)
 
     square = jnp.zeros((ROWS, 1), F32)
     for s in range(SUBS):
@@ -289,11 +402,11 @@
         acc[:, lanes(s)] = part
         square += jnp.sum(part * part, axis=1, keepdims=True)
     scale = lax.rsqrt(square / WIDTH + NORM_EPS)
-    mixed = (res_ref[...].astype(F32) + acc[...] * scale * post_ref[...]).astype(BF16)
+    mixed = (res_ref[...].astype(F32) + acc[...] * scale * whole_row(post_ref)).astype(BF16)
     mixed_ref[...] = mixed
     wide = mixed.astype(F32)
     scale = lax.rsqrt(jnp.sum(wide * wide, axis=1, keepdims=True) / WIDTH + NORM_EPS)
-    x_buf[block(0), :] = (wide * scale * ffn_ref[...]).astype(BF16)
+    x_buf[block(0), :] = (wide * scale * whole_row(ffn_ref)).astype(BF16)
 
     ag_flows = ((0, z_up, -1, (0, 1)), (1, z_dn, 1, (2, 3)))
 
@@ -314,13 +427,37 @@
                     continue
                 src = x_buf.at[block(sign * (k - 1)), lanes(s)]
                 sends.go(remote(src, src, ag_send.at[f, k - 1, s], ag_recv.at[f, k - 1, s], to))
+        if k == 2:
+            w_next(1 - row)
+        if k == 3:
+            w_rest(row, -1)
+            w_rest(row, 1)
+        if k == 5:
+            w_far(1 - row)
+            w_rest(row, 2)
+        if k == 7:
+            w_rest(1 - row, -1)
+            w_rest(1 - row, 1)
     for s in range(SUBS):
         ag_got(HOPS, s)
-    x_out[...] = x_buf[...]
+    w_rest(1 - row, 2)
+    w_last()
+
+    def column(n, carry):
+        both = jnp.dot(
+            x_buf[...], w[:, pl.ds(pl.multiple_of(n * 256, 256), 256)], preferred_element_type=F32
+        )
+        gate, up = both[:, :128], both[:, 128:]
+        hidden_ref[:, pl.ds(pl.multiple_of(n * 128, 128), 128)] = (
+            jax.nn.gelu(gate, approximate=True) * up
+        ).astype(BF16)
+        return carry
+
+    lax.fori_loop(0, TILES, column, 0)
     sends.drain()
 
 
-def attention_half(q, k, v, doc_blocks, residual, post_gain, ffn_gain, out_weight):
+def layer(q, k, v, doc_blocks, residual, post_gain, ffn_gain, out_weight, gate, up):
     vmem = pl.BlockSpec(memory_space=pltpu.VMEM)
     tables = [jnp.asarray(a) for a in rope_tables()]
     half = RING // 2
@@ -329,15 +466,16 @@
         layer_kernel,
         out_shape=(
             jax.ShapeDtypeStruct((ROWS, WIDTH), BF16),
-            jax.ShapeDtypeStruct((TOK, WIDTH), BF16),
+            jax.ShapeDtypeStruct((TOK, COLS), BF16),
         ),
         in_specs=[vmem] * 3
         + [pl.BlockSpec(memory_space=pltpu.SMEM)]
         + [vmem] * 7
-        + [pl.BlockSpec(memory_space=pl.ANY)],
+        + [pl.BlockSpec(memory_space=pl.ANY)] * 3,
         out_specs=(vmem, vmem),
         scratch_shapes=[
             pltpu.VMEM((HEAD, WIDTH), BF16),
+            pltpu.VMEM((16 * SHARD, 2 * COLS), BF16),
             pltpu.VMEM((2, TOK, HALF), BF16),
             pltpu.VMEM((16, TOK, HEAD), BF16),
             pltpu.VMEM((16, TOK, HEAD), BF16),
@@ -359,9 +497,12 @@
             dma((2, half, SUBS)),
             dma((2, half, SUBS)),
             dma((2, half, SUBS)),
+            dma((TILES, 2)),
+            dma((40,)),
+            dma((16, 3)),
         ],
         compiler_params=pltpu.CompilerParams(
-            collective_id=0, has_side_effects=True, vmem_limit_bytes=48 * 1024 * 1024
+            collective_id=0, has_side_effects=True, vmem_limit_bytes=56 * 1024 * 1024
         ),
         cost_estimate=pl.CostEstimate(flops=2_000_000_000, bytes_accessed=8_000_000, transcendentals=0),
     )(
@@ -370,15 +511,13 @@
         v,
         doc_blocks,
         residual,
-        post_gain.reshape(1, WIDTH),
-        ffn_gain.reshape(1, WIDTH),
+        post_gain.reshape(WIDTH // 128, 128),
+        ffn_gain.reshape(WIDTH // 128, 128),
         *tables,
         out_weight,
+        gate,
+        up,
     )
-
-
-def gelu_gate(gate_sum, up_sum):
-    return (jax.nn.gelu(gate_sum, approximate=True) * up_sum).astype(BF16)
 
 
 def per_device(
@@ -393,15 +532,18 @@
     gate_weight,
     up_weight,
 ):
-    both = jnp.concatenate([gate_weight, up_weight], axis=1)
-    whole = lax.all_gather(both, "ctx", axis=0, tiled=True)
-    mixed_stream, rows = attention_half(
-        queries, key_heads, value_heads, doc_blocks, residual, post_gain, ffn_gain, out_weight
+    return layer(
+        queries,
+        key_heads,
+        value_heads,
+        doc_blocks,
+        residual,
+        post_gain,
+        ffn_gain,
+        out_weight,
+        gate_weight,
+        up_weight,
     )
-    columns = gate_weight.shape[1]
-    gate_part = jnp.dot(rows, whole[:, :columns], preferred_element_type=F32)
-    up_part = jnp.dot(rows, whole[:, columns:], preferred_element_type=F32)
-    return (mixed_stream, gelu_gate(gate_part, up_part))
 
 
 def solution(mesh):

time: 143 us -> 112 us (0.78)
  the two profiles are of different devices: /device:TPU:1 before, /device:TPU:26 now
where the time goes in v2:
time: 112 us; the launch traced here: 110 us
  Pallas kernels  106 us (95%)
  local copies, waits for them, and re-layouts  3.37 us (3%)
    pallas_call x1, Pallas kernels, layer(): pl.pallas_call(layer_kernel, out_shape=(jax.ShapeDtypeStruct((ROWS, WIDTH...  106 us
    unnamed x2, local copies, waits for them, and re-layouts  3.37 us

profile of v2, /device:TPU:26, one launch (start us, length us, event | category | flops | bytes accessed | tf_op | source)
XLA Modules:
  0.0 110.3 jit_solution(4646213938938795955)
XLA Ops:
  0.6 106.3 %shard_map.149 = (bf16[16,3584]{1,0:T(8,128)(2,1)}, bf16[256,896]{1,0:T(8,128)(2,1)}) custom-call(bf16[256,256]{1,0:T(8,128)(2,1)} %q_ref.1, bf16[256,128]{1,0:T(8,128)(2,1)} %k_ref.1, bf16[256,128]{1,0:T(8,128)(2,1)} %v_ref.1, s32[6]{0:T(128)} %doc_ref.1, bf16[16,3584]{1,0:T(8,128)(2,1)} %res_ref.1, f32[28,128]{1,0:T(8,128)} %bitcast.2, f32[28,128]{1,0:T(8,128)} %bitcast.3, ...), custom_call_target="tpu_custom_call" | custom-call | flops 2000000000 | bytes 8000000 | tf_op jit(solution)/shard_map/pallas_call | solution.py:465
  106.9 1.6 %copy.18 = bf16[16,3584]{1,0:T(8,128)(2,1)} copy(bf16[16,3584]{1,0:T(8,128)(2,1)} %get-tuple-element.4) | data formatting | bytes 229376
  108.5 1.8 %copy.19 = bf16[256,896]{1,0:T(8,128)(2,1)} copy(bf16[256,896]{1,0:T(8,128)(2,1)} %get-tuple-element.5) | data formatting | bytes 917504

commit v3 on v2

v3 whole, which is shorter than its diff:
```python
import functools
import itertools

import jax
import jax.numpy as jnp
import numpy as np
from jax import lax
from jax.experimental import pallas as pl
from jax.experimental.pallas import tpu as pltpu
from jax.sharding import PartitionSpec as P

MESH = pl.DeviceIdType.MESH
BLOCK = 32
SOFT_CAP = 50.0
NORM_EPS = 1e-06
ROPE_BASE = 10000.0
RING = 16
TOK = 256
HEAD = 256
HALF = 128
WIDTH = 3584
ROWS = 16
SUBS = 4
SUB = WIDTH // SUBS
SHARD = 224
COLS = 896
TILES = COLS // 128
MAIN = 144
REST = SHARD - MAIN
POOL = 36
NEAR = 80
FAR = MAIN - NEAR
F32 = jnp.float32
BF16 = jnp.bfloat16


def rope_tables():
    freq = ROPE_BASE ** (-(np.arange(HALF, dtype=np.float64) * 2.0) / HEAD)
    inner = np.arange(TOK, dtype=np.float64)[:, None] * freq[None, :]
    outer = (np.arange(16, dtype=np.float64) * TOK)[:, None] * freq[None, :]
    return np.concatenate([f(a) for a in (inner, outer) for f in (np.cos, np.sin)]).astype(np.float32)


class Sends:
    def __init__(self):
        self.pending = {}

    @staticmethod
    def under(cond, act):
        if cond is None:
            act()
        else:
            pl.when(cond)(act)

    def go(self, key, copy, cond=None):
        self.settle(key)
        self.under(cond, copy.start)
        self.pending[key] = (copy, cond)

    def settle(self, key):
        if key in self.pending:
            copy, cond = self.pending.pop(key)
            self.under(cond, copy.wait_send)

    def drain(self):
        for key in list(self.pending):
            self.settle(key)


def layer_kernel(
    q_hbm,
    k_hbm,
    v_hbm,
    doc_ref,
    res_hbm,
    post_hbm,
    ffn_hbm,
    tables_hbm,
    ow_hbm,
    gate_hbm,
    up_hbm,
    mixed_hbm,
    hidden_hbm,
    q_ref,
    res_ref,
    post_ref,
    ffn_ref,
    tables,
    mixed_ref,
    hidden_ref,
    ow,
    w,
    rawk,
    kk,
    vv,
    qrot,
    num,
    den,
    term,
    rs_r,
    rs_l,
    acc,
    x_buf,
    load_sem,
    out_sem,
    pair_send,
    pair_recv,
    xy_send,
    k_recv,
    v_recv,
    z_send,
    z_recv,
    w_recv,
    far_recv,
):
    dp = lax.axis_index("dp")
    c = lax.axis_index("ctx")
    t = lax.axis_index("tensor")
    row = c // 8
    x = (c % 8) // 2
    core = c % 2
    par = t % 2

    def at(r, xx, kk_, d=dp):
        return (d, r * 8 + xx * 2 + kk_, t)

    x_up = (x + 1) % 4
    x_dn = (x + 3) % 4
    right_x = at(row, x_up, core)
    left_x = at(row, x_dn, core)
    cross = at(1 - row, x, core)
    sib = at(row, x, 1 - core)
    z_up = (dp, c, (t + 1) % RING)
    z_dn = (dp, c, (t + RING - 1) % RING)
    mate = (dp, c, t + 1 - 2 * par)
    twin = at(row, x, core, 1 - dp)
    other = at(1 - row, x, core, 1 - dp)

    barrier = pltpu.get_barrier_semaphore()
    friends = (right_x, left_x, cross, sib, z_up, z_dn, twin, other)
    for friend in friends:
        pl.semaphore_signal(barrier, inc=1, device_id=friend, device_id_type=MESH)
    own_lanes = pl.ds(pl.multiple_of(par * HALF, HALF), HALF)

    def load(i, src, dst):
        copy = pltpu.make_async_copy(src, dst, load_sem.at[i])
        copy.start()
        return copy

    got_k = load(0, k_hbm, rawk.at[par])
    got_v = load(1, v_hbm, vv.at[c, :, own_lanes])
    got_q = load(2, q_hbm, q_ref)
    got_tables = load(3, tables_hbm, tables)
    got_ow = load(4, ow_hbm, ow)
    got_norm = [
        load(5 + i, src, dst)
        for i, (src, dst) in enumerate(((res_hbm, res_ref), (post_hbm, post_ref), (ffn_hbm, ffn_ref)))
    ]
    own_rows = pl.ds(pl.multiple_of(c * SHARD, 16), SHARD)
    for n in range(TILES):
        for i, ref in enumerate((gate_hbm, up_hbm)):
            pltpu.make_async_copy(
                ref.at[:, pl.ds(n * 128, 128)],
                w.at[own_rows, pl.ds(n * 256 + i * 128, 128)],
                load_sem.at[8],
            ).start()

    sends = Sends()

    def remote(src, dst, send, recv, to):
        return pltpu.make_async_remote_copy(
            src_ref=src, dst_ref=dst, send_sem=send, recv_sem=recv, device_id=to, device_id_type=MESH
        )

    def attend(b, n):
        lane = b * TOK + lax.broadcasted_iota(jnp.int32, (1, n * TOK), 1)
        keys = kk[pl.ds(b, n)].reshape(n * TOK, HEAD)
        values = vv[pl.ds(b, n)].reshape(n * TOK, HEAD)
        scores = lax.dot_general(qrot[...], keys, (((1,), (1,)), ((), ())), preferred_element_type=F32)
        capped = jnp.tanh(scores * (1.0 / (SOFT_CAP * HEAD**0.5))) * (SOFT_CAP / np.log(2.0))
        visible = (lane >= begin) & (lane <= qpos)
        weights = jnp.where(visible, jnp.exp2(capped), 0.0).astype(BF16)
        wide = weights.astype(F32)
        den[...] += functools.reduce(
            jnp.add, [wide[:, i * HALF : (i + 1) * HALF] for i in range(n * TOK // HALF)]
        )
        num[...] += jnp.dot(weights, values, preferred_element_type=F32)

    got_k.wait()
    got_v.wait()
    with jax.named_scope("bar"):
        pl.semaphore_wait(barrier, len(friends))
    pair_k = remote(rawk.at[par], rawk.at[par], pair_send.at[0], pair_recv.at[0], mate)
    own_v = vv.at[c, :, own_lanes]
    pair_v = remote(own_v, own_v, pair_send.at[1], pair_recv.at[1], mate)
    sends.go("pair_k", pair_k)
    sends.go("pair_v", pair_v)

    got_tables.wait()
    cb = tables[pl.ds(2 * TOK + c, 1), :]
    sb = tables[pl.ds(2 * TOK + 16 + c, 1), :]
    cosine = tables[:TOK, :] * cb - tables[TOK : 2 * TOK, :] * sb
    sine = tables[TOK : 2 * TOK, :] * cb + tables[:TOK, :] * sb

    def turned(a, b, where):
        a, b = a.astype(F32), b.astype(F32)
        where[:, :HALF] = (a * cosine - b * sine).astype(BF16)
        where[:, HALF:] = (b * cosine + a * sine).astype(BF16)

    got_q.wait()
    turned(q_ref[:, :HALF], q_ref[:, HALF:], qrot)
    num[...] = jnp.zeros_like(num)
    den[...] = jnp.zeros_like(den)

    qpos = c * TOK + lax.broadcasted_iota(jnp.int32, (TOK, 1), 0)
    begin = jnp.zeros((TOK, 1), jnp.int32)
    total = 0
    for e in range(5):
        total = total + doc_ref[e]
        edge = total * BLOCK
        begin = jnp.where(qpos >= edge, jnp.maximum(begin, edge), begin)


    slot = itertools.cycle(range(POOL))

    def kv_go(ref, recv, b, to, cond):
        i = next(slot)
        sends.go(i, remote(ref.at[b], ref.at[b], xy_send.at[i], recv.at[b], to), cond)

    both = ((kk, k_recv), (vv, v_recv))

    def kv_wait(ref, recv, b, cond):
        got = remote(ref.at[b], ref.at[b], xy_send.at[0], recv.at[b], sib)
        pl.when(cond)(got.wait_recv)

    def spread(ref, recv):
        kv_go(ref, recv, c, cross, row == 0)
        kv_go(ref, recv, c, right_x, x < 3)
        kv_go(ref, recv, c, left_x, x == 0)
        kv_go(ref, recv, c, sib, core == 0)

    with jax.named_scope("pairk"):
        pair_k.wait_recv()
    turned(rawk[0], rawk[1], kk.at[c])
    spread(*both[0])
    with jax.named_scope("pairv"):
        pair_v.wait_recv()
    spread(*both[1])

    mid = (x == 1) | (x == 2)
    lower = row == 1
    even = c - core
    clip = lambda b: jnp.clip(b, 0, 15)

    def come(b, here, onward):
        for ref, recv in both:
            kv_wait(ref, recv, b, here)
            for to, cond in onward:
                kv_go(ref, recv, b, to, cond)

    def attend_pair(first, here):
        theirs = first + 1 - core
        for ref, recv in both:
            kv_wait(ref, recv, theirs, here)
        pl.when(here)(lambda: attend(first, 2))

    def right_going(hop):
        onward = ((right_x, mid),) if hop == 1 else ()
        come(clip(c - 2 * hop), x >= hop, onward + ((sib, x >= hop),))

    def left_going(hop):
        here = lower & (x + hop <= 3)
        onward = ((left_x, lower & mid),) if hop == 1 else ()
        come(clip(c - 8 + 2 * hop), here, onward + ((sib, here),))

    def attend_right(hop):
        attend_pair(clip(even - 2 * hop), x >= hop)

    def attend_left(hop):
        attend_pair(clip(even - 8 + 2 * hop), lower & (x + hop <= 3))

    def shard(r, dx, plane=core):
        return r * 8 + ((x + dx) % 4) * 2 + plane

    def cut(b, start, size):
        return w.at[pl.ds(pl.multiple_of(b * SHARD + start, 16), size), :]

    def w_sem(b, kind):
        return far_recv.at[b // 8] if kind == 2 else w_recv.at[b, kind]

    def w_go(b, start, size, kind, to, cond=None):
        ref = cut(b, start, size)
        i = next(slot)
        sends.go(i, remote(ref, ref, xy_send.at[i], w_sem(b, kind), to), cond)

    def w_wait(b, size, kind):
        ref = cut(b, 0, size)
        remote(ref, ref, xy_send.at[0], w_sem(b, kind), sib).wait_recv()

    main_at = REST * dp
    rest_at = MAIN * dp
    twin_main_at = REST * (1 - dp)
    twin_rest_at = MAIN * (1 - dp)

    def w_across(cond):
        b = shard(row, 0)
        w_go(b, twin_main_at, MAIN, 0, other, cond)
        w_go(b, rest_at, REST, 1, other, cond)

    mine = cut(shard(row, 0), 0, SHARD)
    pltpu.make_async_copy(mine, mine, load_sem.at[8]).wait()
    w_across(lower)
    with jax.named_scope("own"):
        pl.when(core == 0)(lambda: attend(c, 1))
        attend_pair(even, core == 1)
    with jax.named_scope("right1"):
        right_going(1)
    with jax.named_scope("cross"):
        come(
            clip(c - 8),
            lower,
            ((left_x, lower & (x > 0)), (right_x, lower & (x == 3)), (sib, lower & (core == 1))),
        )
    with jax.named_scope("attR1"):
        attend_right(1)
    with jax.named_scope("left1"):
        left_going(1)
    with jax.named_scope("right2"):
        right_going(2)
    with jax.named_scope("right3"):
        right_going(3)
    with jax.named_scope("left3"):
        left_going(3)
    with jax.named_scope("attX"):
        attend_pair(clip(even - 8), lower & (core == 0))
        pl.when(lower & (core == 1))(lambda: attend(clip(c - 8), 1))
    with jax.named_scope("attL1"):
        attend_left(1)
    with jax.named_scope("left2"):
        left_going(2)
    with jax.named_scope("att"):
        attend_right(2)
        attend_right(3)
        attend_left(3)
        attend_left(2)

    def w_first():
        b = shard(row, 0)
        w_across(row == 0)
        w_go(b, main_at, MAIN, 0, right_x)
        w_go(b, main_at, MAIN, 0, left_x)
        w_go(b, 0, SHARD, 0, sib)

    def w_cross():
        b = shard(1 - row, 0)
        w_wait(b, MAIN, 0)
        w_go(b, main_at, MAIN, 0, right_x)
        w_go(b, main_at, MAIN, 0, left_x)
        w_go(b, main_at, MAIN, 0, sib)

    def w_cross_rest():
        b = shard(1 - row, 0)
        w_wait(b, REST, 1)
        w_go(b, twin_rest_at, REST, 1, sib)

    def w_next(r):
        for dx, to, start, size, kind in ((-1, right_x, 0, NEAR, 0), (1, left_x, NEAR, FAR, 2)):
            b = shard(r, dx)
            w_wait(b, MAIN, 0)
            w_go(b, main_at + start, size, kind, to)
            w_go(b, rest_at, REST, 1, at((row + r) % 2, x, core, 1 - dp))
            w_go(b, main_at, MAIN, 0, sib)

    def w_far(r):
        b = shard(r, 2)
        w_wait(b, NEAR, 0)
        w_wait(b, FAR, 2)
        w_go(b, rest_at, REST, 1, twin)
        w_go(b, main_at, MAIN, 0, sib)

    def w_rest(r, dx):
        b = shard(r, dx)
        w_wait(b, REST, 1)
        w_go(b, twin_rest_at, REST, 1, sib)

    def w_last():
        for r in (row, 1 - row):
            for dx in (0, -1, 1, 2):
                b = shard(r, dx, 1 - core)
                if dx == 0 and r is row:
                    w_wait(b, SHARD, 0)
                else:
                    w_wait(b, MAIN, 0)
                    w_wait(b, REST, 1)

    events = {
        ("rs", 4): (lambda: w_next(row),),
        ("rs", 5): (w_cross,),
        ("rs", 6): (lambda: w_far(row),),
        ("rs", 7): (w_cross_rest,),
        ("ag", 2): (lambda: w_next(1 - row),),
        ("ag", 4): (lambda: w_far(1 - row),),
        ("ag", 5): (lambda: w_rest(row, -1), lambda: w_rest(row, 1)),
        ("ag", 7): (lambda: w_rest(row, 2), lambda: w_rest(1 - row, -1), lambda: w_rest(1 - row, 1)),
        ("ag", 8): (lambda: w_rest(1 - row, 2),),
    }
    w_first()
    got_ow.wait()
    sums = jnp.sum(den[...], axis=1, keepdims=True)
    attended = (num[...] / sums).astype(BF16)

    def lanes(s):
        return pl.ds(s * SUB, SUB)

    def block(d):
        return pl.ds(pl.multiple_of(lax.rem(t + d + RING, RING) * ROWS, ROWS), ROWS)

    HOPS = RING // 2
    flows = (
        (0, rs_r, z_up, 1, range(SUBS // 2)),
        (1, rs_l, z_dn, -1, range(SUBS // 2, SUBS)),
    )

    def rs_step(k, s):
        for f, buf, to, sign, early in flows:
            begin_at = 1 if s in early else 2
            if k < begin_at:
                continue
            away = sign * (HOPS + 1 - k)
            if k == begin_at:
                src = term.at[block(away), lanes(s)]
            else:
                src = buf.at[k - 2, :, lanes(s)]
                remote(src, src, z_send.at[f, s], z_recv.at[f, k - 2, s], to).wait_recv()
                buf[k - 2, :, lanes(s)] = (
                    buf[k - 2, :, lanes(s)].astype(F32) + term[block(away), lanes(s)].astype(F32)
                ).astype(BF16)
            sends.go(
                ("z", f, s),
                remote(src, buf.at[k - 1, :, lanes(s)], z_send.at[f, s], z_recv.at[f, k - 1, s], to),
            )

    for s in range(SUBS):
        term[:, lanes(s)] = jnp.dot(attended, ow[:, lanes(s)], preferred_element_type=F32).astype(BF16)
        rs_step(1, s)
    for k in range(2, HOPS + 1):
        with jax.named_scope(f"rs{k}"):
            for s in range(SUBS):
                rs_step(k, s)
        with jax.named_scope(f"rsw{k}"):
            for act in events.get(("rs", k), ()):
                act()

    def whole_row(ref):
        return jnp.concatenate([ref[i : i + 1, :] for i in range(WIDTH // 128)], axis=1)

    for one in got_norm:
        one.wait()
    square = jnp.zeros((ROWS, 1), F32)
    for s in range(SUBS):
        for f, buf, to, _, _ in flows:
            src = buf.at[HOPS - 1, :, lanes(s)]
            remote(src, src, z_send.at[f, s], z_recv.at[f, HOPS - 1, s], to).wait_recv()
        part = (
            term[block(0), lanes(s)].astype(F32)
            + rs_r[HOPS - 1, :, lanes(s)].astype(F32)
            + rs_l[HOPS - 1, :, lanes(s)].astype(F32)
        )
        acc[:, lanes(s)] = part
        square += jnp.sum(part * part, axis=1, keepdims=True)
    scale = lax.rsqrt(square / WIDTH + NORM_EPS)
    mixed = (res_ref[...].astype(F32) + acc[...] * scale * whole_row(post_ref)).astype(BF16)
    mixed_ref[...] = mixed
    mixed_out = pltpu.make_async_copy(mixed_ref, mixed_hbm, out_sem.at[1])
    mixed_out.start()
    wide = mixed.astype(F32)
    scale = lax.rsqrt(jnp.sum(wide * wide, axis=1, keepdims=True) / WIDTH + NORM_EPS)
    x_buf[block(0), :] = (wide * scale * whole_row(ffn_ref)).astype(BF16)

    ag_flows = ((0, z_up, -1, range(SUBS // 2)), (1, z_dn, 1, range(SUBS // 2, SUBS)))

    def ag_got(k, s):
        for f, to, sign, late in ag_flows:
            if k == HOPS and s not in late:
                continue
            src = x_buf.at[block(sign * k), lanes(s)]
            remote(src, src, z_send.at[f, s], z_recv.at[f, k - 1, s], to).wait_recv()

    for k in range(1, HOPS + 1):
        with jax.named_scope(f"ag{k}"):
            for s in range(SUBS):
                for f, to, sign, late in ag_flows:
                    if k > 1:
                        got = x_buf.at[block(sign * (k - 1)), lanes(s)]
                        remote(got, got, z_send.at[f, s], z_recv.at[f, k - 2, s], to).wait_recv()
                    if k == HOPS and s not in late:
                        continue
                    src = x_buf.at[block(sign * (k - 1)), lanes(s)]
                    sends.go(("z", f, s), remote(src, src, z_send.at[f, s], z_recv.at[f, k - 1, s], to))
        with jax.named_scope(f"agw{k}"):
            for act in events.get(("ag", k), ()):
                act()
    with jax.named_scope("aglast"):
        for s in range(SUBS):
            ag_got(HOPS, s)
    with jax.named_scope("wlast"):
        w_last()

    with jax.named_scope("ffn"):
        for n in range(TILES):
            both_parts = jnp.dot(x_buf[...], w[:, pl.ds(n * 256, 256)], preferred_element_type=F32)
            gate, up = both_parts[:, :128], both_parts[:, 128:]
            tile = pl.ds(n * 128, 128)
            hidden_ref[:, tile] = (jax.nn.gelu(gate, approximate=True) * up).astype(BF16)
            out = pltpu.make_async_copy(hidden_ref.at[:, tile], hidden_hbm.at[:, tile], out_sem.at[0])
            out.start()
    with jax.named_scope("drain"):
        sends.drain()
        mixed_out.wait()
        pltpu.make_async_copy(hidden_ref, hidden_hbm, out_sem.at[0]).wait()


def layer(q, k, v, doc_blocks, residual, post_gain, ffn_gain, out_weight, gate, up):
    hbm = pl.BlockSpec(memory_space=pl.ANY)
    half = RING // 2
    dma = pltpu.SemaphoreType.DMA
    vmem = pltpu.VMEM
    return pl.pallas_call(
        layer_kernel,
        out_shape=(
            jax.ShapeDtypeStruct((ROWS, WIDTH), BF16),
            jax.ShapeDtypeStruct((TOK, COLS), BF16),
        ),
        in_specs=[hbm] * 3 + [pl.BlockSpec(memory_space=pltpu.SMEM)] + [hbm] * 7,
        out_specs=(hbm, hbm),
        scratch_shapes=[
            vmem((TOK, HEAD), BF16),
            vmem((ROWS, WIDTH), BF16),
            vmem((WIDTH // 128, 128), F32),
            vmem((WIDTH // 128, 128), F32),
            vmem((2 * TOK + 32, HALF), F32),
            vmem((ROWS, WIDTH), BF16),
            vmem((TOK, COLS), BF16),
            vmem((HEAD, WIDTH), BF16),
            vmem((16 * SHARD, 2 * COLS), BF16),
            vmem((2, TOK, HALF), BF16),
            vmem((16, TOK, HEAD), BF16),
            vmem((16, TOK, HEAD), BF16),
            vmem((TOK, HEAD), BF16),
            vmem((TOK, HEAD), F32),
            vmem((TOK, HALF), F32),
            vmem((TOK, WIDTH), BF16),
            vmem((half, ROWS, WIDTH), BF16),
            vmem((half, ROWS, WIDTH), BF16),
            vmem((ROWS, WIDTH), F32),
            vmem((TOK, WIDTH), BF16),
            dma((9,)),
            dma((2,)),
            dma((2,)),
            dma((2,)),
            dma((POOL,)),
            dma((16,)),
            dma((16,)),
            dma((2, SUBS)),
            dma((2, half, SUBS)),
            dma((16, 2)),
            dma((2,)),
        ],
        compiler_params=pltpu.CompilerParams(
            collective_id=0, has_side_effects=True, vmem_limit_bytes=56 * 1024 * 1024
        ),
        cost_estimate=pl.CostEstimate(flops=2_000_000_000, bytes_accessed=8_000_000, transcendentals=0),
    )(
        q,
        k,
        v,
        doc_blocks,
        residual,
        post_gain.reshape(WIDTH // 128, 128),
        ffn_gain.reshape(WIDTH // 128, 128),
        jnp.asarray(rope_tables()),
        out_weight,
        gate,
        up,
    )


def per_device(
    residual,
    queries,
    key_heads,
    value_heads,
    doc_blocks,
    out_weight,
    post_gain,
    ffn_gain,
    gate_weight,
    up_weight,
):
    return layer(
        queries,
        key_heads,
        value_heads,
        doc_blocks,
        residual,
        post_gain,
        ffn_gain,
        out_weight,
        gate_weight,
        up_weight,
    )


def solution(mesh):
    in_specs = (
        P(("dp", "ctx", "tensor"), None),
        P(("dp", "ctx"), "tensor"),
        P(("dp", "ctx"), "tensor"),
        P(("dp", "ctx"), "tensor"),
        P("dp"),
        P("tensor", None),
        P(),
        P(),
        P("ctx", "tensor"),
        P("ctx", "tensor"),
    )
    out_specs = (P(("dp", "ctx", "tensor"), None), P(("dp", "ctx"), "tensor"))
    return jax.shard_map(
        per_device, mesh=mesh, in_specs=in_specs, out_specs=out_specs, check_vma=False
    )
```

time: 112 us -> 103 us (0.920)
  the two profiles are of different devices: /device:TPU:26 before, /device:TPU:20 now
where the time goes in v3:
time: 103 us; the launch traced here: 102 us
  Pallas kernels  98.3 us (95%)
  local copies, waits for them, and re-layouts  3.37 us (3%)
    pallas_call x1, Pallas kernels, layer(): pl.pallas_call(layer_kernel, out_shape=(jax.ShapeDtypeStruct((ROWS, WIDTH...  98.3 us
    unnamed x2, local copies, waits for them, and re-layouts  3.37 us

profile of v3, /device:TPU:20, one launch (start us, length us, event | category | flops | bytes accessed | tf_op | source)
XLA Modules:
  0.0 102.4 jit_solution(13073337918177329811)
XLA Ops:
  0.6 98.3 %shard_map.122 = (bf16[16,3584]{1,0:T(8,128)(2,1)}, bf16[256,896]{1,0:T(8,128)(2,1)}) custom-call(bf16[256,256]{1,0:T(8,128)(2,1)} %q_hbm.1, bf16[256,128]{1,0:T(8,128)(2,1)} %k_hbm.1, bf16[256,128]{1,0:T(8,128)(2,1)} %v_hbm.1, s32[6]{0:T(128)} %doc_ref.1, bf16[16,3584]{1,0:T(8,128)(2,1)} %res_hbm.1, f32[28,128]{1,0:T(8,128)} %bitcast.2, f32[28,128]{1,0:T(8,128)} %bitcast.3, ...), custom_call_target="tpu_custom_call" | custom-call | flops 2000000000 | bytes 8000000 | tf_op jit(solution)/shard_map/pallas_call | solution.py:528
  99.0 1.6 %copy.15 = bf16[16,3584]{1,0:T(8,128)(2,1)} copy(bf16[16,3584]{1,0:T(8,128)(2,1)} %get-tuple-element.4) | data formatting | bytes 229376
  100.5 1.8 %copy.16 = bf16[256,896]{1,0:T(8,128)(2,1)} copy(bf16[256,896]{1,0:T(8,128)(2,1)} %get-tuple-element.5) | data formatting | bytes 917504
